TPU v7x, 32 devices: a whole 2x2x4 slice. The times are simulated.
32 devices in a mesh: dp: 4 (over x, y), ep: 8 (over z, core).
Axes of the slice: x: 2, y: 2, z: 4, core: 2. Of those that a mesh axis runs over, the one named last changes fastest.
Arguments:
- tokens: bfloat16 [8192, 2048], P(('dp', 'ep')), parts along dimension 0
- expert_ids: int32 [8192, 6], P(('dp', 'ep')), parts along dimension 0
- gate_vals: float32 [8192, 6], P(('dp', 'ep')), parts along dimension 0
- w_gate: bfloat16 [64, 2048, 1408], P('ep')
- w_up: bfloat16 [64, 2048, 1408], P('ep')
- w_down: bfloat16 [64, 1408, 2048], P('ep')
Outputs:
- output: bfloat16 [8192, 2048], P(('dp', 'ep')), parts along dimension 0
There are 4 independent parts. A program takes and returns all parts, laid end to end along the dimension named above; an argument that names none is the same for every part.
All inputs are finite; a program needn't handle non-finite values.
Results may differ from a plain program's by a relative error of at most 0.00665691.
Values are sent between devices in bfloat16 or wider.
A program may use at most 1 GiB of HBM per device.

v0:
```python
import jax
import jax.numpy as jnp
from jax import lax
from jax.sharding import PartitionSpec as P, NamedSharding


def expert_ffn(expert_in, w_gate, w_up, w_down):
    gate_act = jnp.einsum('lcd,ldf->lcf', expert_in, w_gate, preferred_element_type=jnp.float32)
    up_act = jnp.einsum('lcd,ldf->lcf', expert_in, w_up, preferred_element_type=jnp.float32)
    hidden = (jax.nn.silu(gate_act) * up_act).astype(jnp.bfloat16)
    return jnp.einsum('lcf,lfd->lcd', hidden, w_down, preferred_element_type=jnp.float32).astype(jnp.bfloat16)


def serve_rows(recv_rows, recv_gate, w_gate, w_up, w_down, expert_cap):
    member = recv_gate != 0.0
    exp_slot = jnp.cumsum(member.astype(jnp.int32), axis=0) - 1
    fan_mat = (member.T[:, None, :] & (exp_slot.T[:, None, :] == jnp.arange(expert_cap)[None, :, None])).astype(jnp.bfloat16)
    expert_in = jnp.einsum('lcr,rd->lcd', fan_mat, recv_rows, preferred_element_type=jnp.float32).astype(jnp.bfloat16)
    expert_out = expert_ffn(expert_in, w_gate, w_up, w_down)
    row_outs = jnp.einsum('lcr,lcd->lrd', fan_mat, expert_out, preferred_element_type=jnp.float32)
    dev_sum = jnp.sum(recv_gate.T[:, :, None] * row_outs, axis=0)
    return dev_sum.astype(jnp.bfloat16)


def send_tables(expert_ids, gate_vals, groups, local_count, pair_cap):
    tok_dev = expert_ids.shape[0]
    chosen = jnp.any((expert_ids // local_count)[:, :, None] == jnp.arange(groups)[None, None, :], axis=1)
    send_rank = jnp.cumsum(chosen.astype(jnp.int32), axis=0) - 1
    pack_mask = chosen.T[:, None, :] & (send_rank.T[:, None, :] == jnp.arange(pair_cap)[None, :, None])
    gate_dense = jnp.sum(jnp.where(expert_ids[:, :, None] == jnp.arange(groups * local_count)[None, None, :], gate_vals[:, :, None], 0.0), axis=1)
    gate_t = jnp.swapaxes(gate_dense.reshape(tok_dev, groups, local_count), 0, 1)
    send_gate = jnp.sum(jnp.where(pack_mask[:, :, :, None], gate_t[:, None, :, :], 0.0), axis=2)
    return pack_mask.astype(jnp.bfloat16), send_gate


def solution(mesh):
    groups = mesh.shape['ep']
    row_spec = P(('dp', 'ep'))
    expert_spec = P('ep')

    def device_step(tokens, expert_ids, gate_vals, w_gate, w_up, w_down):
        tok_dev, top_k = expert_ids.shape
        d_model = tokens.shape[1]
        local_count = w_gate.shape[0]
        pair_cap = tok_dev * (top_k // 2) // groups
        expert_cap = tok_dev * top_k // local_count
        row_count = groups * pair_cap
        pack_mat, send_gate = send_tables(expert_ids, gate_vals, groups, local_count, pair_cap)
        send_rows = jnp.einsum('qct,td->qcd', pack_mat, tokens, preferred_element_type=jnp.float32).astype(jnp.bfloat16)
        recv_rows = lax.all_to_all(send_rows, 'ep', 0, 0, tiled=True)
        recv_gate = lax.all_to_all(send_gate, 'ep', 0, 0, tiled=True)
        dev_sum = serve_rows(recv_rows.reshape(row_count, d_model), recv_gate.reshape(row_count, local_count), w_gate, w_up, w_down, expert_cap)
        returned = lax.all_to_all(dev_sum.reshape(groups, pair_cap, d_model), 'ep', 0, 0, tiled=True)
        moe_sum = jnp.einsum('qct,qcd->td', pack_mat, returned, preferred_element_type=jnp.float32)
        return (tokens.astype(jnp.float32) + moe_sum).astype(jnp.bfloat16)

    return jax.shard_map(device_step, mesh=mesh, in_specs=(row_spec, row_spec, row_spec, expert_spec, expert_spec, expert_spec), out_specs=row_spec, check_vma=False)
```

profile of v0, /device:TPU:0, one launch (start us, length us, event | category | flops | bytes accessed | tf_op | source)
XLA Modules:
  0.0 245.8 jit_solution(5792523489515802156)
XLA Ops:
  0.0 0.7 add_select_fusion
  0.7 0.6 reduce-window.14
  1.3 0.2 slice_reduce_fusion
  1.6 0.1 add_bitcast_fusion.1
  1.7 0.8 select_reduce_fusion.1
  2.4 0.1 fusion.17
  2.6 1.0 select_reduce_fusion
  3.6 0.8 copy.31
  4.3 6.4 %all-to-all-start = ((f32[8,96,8]{1,2,0:T(8,128)}), f32[8,96,8]{1,2,0:T(8,128)S(1)}, u32[]{:S(2)}, u32[]{:S(2)}) async-start(f32[8,96,8]{1,2,0:T(8,128)} %copy.31), calls=%async_computation | async-start | bytes 65536 | tf_op jit(solution)/shard_map/all_to_all | solution.py:51
  10.7 3.9 %convolution_convert_fusion = bf16[8,96,2048]{2,1,0:T(8,128)(2,1)} fusion(bf16[256,2048]{1,0:T(8,128)(2,1)} %param.6, s32[8,256]{1,0:T(8,128)S(1)} %add_bitcast_fusion.1, pred[8,256]{1,0:T(8,128)(4,1)S(1)} %bitcast.47), kind=kOutput, calls=%fused_computation.9 | convolution fusion | flops 807272448 | bytes 4204544 | tf_op jit(solution)/shard_map/qct,td->qcd/dot_general | solution.py:49
  14.6 1.7 all-to-all-done
  16.2 3.8 %all-to-all-start.1 = ((bf16[8,96,2048]{2,1,0:T(8,128)(2,1)}), bf16[8,96,2048]{2,1,0:T(8,128)(2,1)S(1)}, u32[]{:S(2)}, u32[]{:S(2)}) async-start(bf16[8,96,2048]{2,1,0:T(8,128)(2,1)} %convolution_convert_fusion), calls=%async_computation.1 | async-start | bytes 6291456 | tf_op jit(solution)/shard_map/all_to_all | solution.py:50
  20.1 0.1 reshape.58
  20.2 1.7 reduce-window.16
  21.9 0.1 slice.17
  22.0 0.1 copy.33
  22.1 0.2 reduce-window.19
  22.3 0.1 copy.34
  22.4 0.1 add_bitcast_fusion
  22.4 68.7 %all-to-all-done.1 = bf16[8,96,2048]{2,1,0:T(8,128)(2,1)S(1)} async-done(((bf16[8,96,2048]{2,1,0:T(8,128)(2,1)}), bf16[8,96,2048]{2,1,0:T(8,128)(2,1)S(1)}, u32[]{:S(2)}, u32[]{:S(2)}) %all-to-all-start.1) | async-done | bytes 3145760 | tf_op jit(solution)/shard_map/all_to_all | solution.py:50
  91.1 6.9 %fusion.7 = bf16[8,192,2048]{2,1,0:T(8,128)(2,1)} fusion(bf16[768,2048,1]{1,0,2:T(8,128)(2,1)S(1)} %bitcast.42, s32[8,768]{1,0:T(8,128)S(1)} %add_bitcast_fusion, pred[8,768]{1,0:T(8,128)(4,1)S(1)} %get-tuple-element.6), kind=kOutput, calls=%fused_computation.8 | convolution fusion | flops 4837343232 | bytes 9467904 | tf_op jit(solution)/shard_map/lcr,rd->lcd/dot_general | solution.py:18
  98.1 22.2 %fusion.23 = f32[8,192,1408]{2,1,0:T(8,128)} fusion(bf16[8,192,2048]{2,1,0:T(8,128)(2,1)} %fusion.7, bf16[8,2048,1408]{2,1,0:T(8,128)(2,1)} %param.9), kind=kOutput, calls=%fused_computation.37 | convolution fusion | flops 8858370048 | bytes 61079552 | tf_op jit(solution)/shard_map/lcd,ldf->lcf/dot_general | solution.py:8
  120.3 25.2 %multiply_convert_fusion = bf16[8,192,1408]{2,1,0:T(8,128)(2,1)} fusion(f32[8,192,1408]{2,1,0:T(8,128)} %fusion.23, bf16[8,192,2048]{2,1,0:T(8,128)(2,1)} %fusion.7, bf16[8,2048,1408]{2,1,0:T(8,128)(2,1)} %param.10), kind=kOutput, calls=%fused_computation.1 | convolution fusion | flops 8871346176 | bytes 65404928 | tf_op jit(solution)/shard_map/lcd,ldf->lcf/dot_general | solution.py:9
  145.5 24.1 %multiply_reduce_fusion = bf16[768,2048]{1,0:T(8,128)(2,1)S(1)} fusion(f32[8,768]{1,0:T(8,128)S(1)} %bitcast.45, bf16[8,192,1408]{2,1,0:T(8,128)(2,1)} %multiply_convert_fusion, bf16[8,1408,2048]{2,1,0:T(8,128)(2,1)} %param.11, s32[8,768]{1,0:T(8,128)S(1)} %add_bitcast_fusion, pred[8,768]{1,0:T(8,128)(4,1)S(1)} %get-tuple-element.6), kind=kOutput, calls=%fused_computation | convolution fusion | flops 13719306240 | bytes 53663744 | tf_op jit(solution)/shard_map/lcr,lcd->lrd/dot_general | solution.py:20
  169.6 0.0 copy-start
  169.6 74.2 %all_to_all.15 = bf16[8,96,2048]{2,1,0:T(8,128)(2,1)S(1)} all-to-all(bf16[8,96,2048]{2,1,0:T(8,128)(2,1)S(1)} %bitcast.43), channel_id=1, replica_groups=mesh['dp'=4,'ep'=8] {'ep'}, dimensions={0} | all-to-all | bytes 6291456 | tf_op jit(solution)/shard_map/all_to_all | solution.py:53
  243.8 0.0 copy-done
  243.8 2.0 fusion.11
  (6 shorter events, 0.1 us)
Async XLA Ops:
  4.3 11.9 %all-to-all-start = ((f32[8,96,8]{1,2,0:T(8,128)}), f32[8,96,8]{1,2,0:T(8,128)S(1)}, u32[]{:S(2)}, u32[]{:S(2)}) async-start(f32[8,96,8]{1,2,0:T(8,128)} %copy.31), calls=%async_computation | async-start | bytes 65536 | tf_op jit(solution)/shard_map/all_to_all | solution.py:51
  16.2 74.9 %all-to-all-start.1 = ((bf16[8,96,2048]{2,1,0:T(8,128)(2,1)}), bf16[8,96,2048]{2,1,0:T(8,128)(2,1)S(1)}, u32[]{:S(2)}, u32[]{:S(2)}) async-start(bf16[8,96,2048]{2,1,0:T(8,128)(2,1)} %convolution_convert_fusion), calls=%async_computation.1 | async-start | bytes 6291456 | tf_op jit(solution)/shard_map/all_to_all | solution.py:50
  169.6 74.2 %copy-start = (bf16[256,2048]{1,0:T(8,128)(2,1)S(1)}, bf16[256,2048]{1,0:T(8,128)(2,1)}, u32[]{:S(2)}) copy-start(bf16[256,2048]{1,0:T(8,128)(2,1)} %param.6) | copy-start | bytes 3145732
where the time goes:
time: 246 us
  matrix products  84.4 us (34%)
  blocking collectives  74.2 us (30%)
  waiting for transfers between devices  70.4 us (29%)
  starting transfers between devices  10.2 us (4%)
  other arithmetic  5.28 us (2%)
    all_to_all x1, blocking collectives, device_step(): lax.all_to_all(dev_sum.reshape(groups, pair_cap, d_model), 'ep', 0, 0, ti...  74.2 us
    all_to_all x1, waiting for transfers between devices, device_step(): recv_rows = lax.all_to_all(send_rows, 'ep', 0, 0, tiled=True)  68.7 us
    dot_general x1, matrix products, expert_ffn(): jnp.einsum('lcd,ldf->lcf', expert_in, w_up, preferred_element_type=jnp.fl...  25.2 us
    dot_general x1, matrix products, serve_rows(): jnp.einsum('lcr,lcd->lrd', fan_mat, expert_out, preferred_element_type=jn...  24.1 us
    dot_general x1, matrix products, expert_ffn(): jnp.einsum('lcd,ldf->lcf', expert_in, w_gate, preferred_element_type=jnp....  22.2 us
    dot_general x1, matrix products, serve_rows(): jnp.einsum('lcr,rd->lcd', fan_mat, recv_rows, preferred_element_type=jnp....  6.95 us
    all_to_all x1, starting transfers between devices, device_step(): recv_gate = lax.all_to_all(send_gate, 'ep', 0, 0, tiled=True)  6.39 us
  transfers between devices with their start and end apart: 2, of which 2 were waited for; matrix products, arithmetic and copies ran while one was open for 3% of the time, Pallas kernels for 0%

commit v1 on v0

v1 whole, which is shorter than its diff:
```python
import functools

import jax
import jax.numpy as jnp
from jax import lax
from jax.experimental import pallas as pl
from jax.experimental.pallas import tpu as pltpu
from jax.sharding import PartitionSpec as P

MESH = pl.DeviceIdType.MESH
F32, BF16 = jnp.float32, jnp.bfloat16
WC = 256
WO = 256
DEPTH = 4
DEPTH2 = 6
FAR = 255.0


def flip(me, d):
    z, c = me // 2, me % 2
    hi, lo = z // 2, z % 2
    if d & 4:
        hi = 1 - hi
    if d & 2:
        lo = 1 - lo
    if d & 1:
        c = 1 - c
    return hi * 4 + lo * 2 + c


def dot(a, b):
    return jnp.dot(a, b, preferred_element_type=F32)


def dot_tn(a, b):
    return lax.dot_general(a, b, (((0,), (0,)), ((), ())), preferred_element_type=F32)


def dot_nt(a, b):
    return lax.dot_general(a, b, (((1,), (1,)), ((), ())), preferred_element_type=F32)


def iota(shape, dim):
    return lax.broadcasted_iota(jnp.int32, shape, dim)


def split3(g):
    hi = g.astype(BF16).astype(F32)
    rest = g - hi
    mid = rest.astype(BF16).astype(F32)
    return jnp.concatenate([hi, mid, rest - mid], axis=0).astype(BF16)


def kernel(tok, ids, gate, wg_hbm, wu_hbm, wd_hbm, out,
           near, raw, rly, xb, ret, accg, accu, hid, fan, fan_t, gb, ssum, pk, pt, pos, rpos, gsend, gtab,
           wg, wu, wd,
           raw_s, raw_r, near_s, rly_s, x_r, tab_s, tab_r, pos_s, pos_r, out_s, ret_r, w_s, wd_s):
    n_exp = accg.shape[0]
    cap = accg.shape[1]
    t_dev = tok.shape[0]
    n_ch, rows, _ = xb.shape
    n_out = ret.shape[0]
    pair = rows // 8
    top_k = ids.shape[0]

    me = lax.axis_index("ep")
    core = me % 2
    side = me // 4
    lo = (me // 2) % 2
    is_mid = (lo + side) == 1
    relay_dev = (2 - side) * 2 + core
    far = 1 - side
    far_src = ((3 * far) * 2 + core, (1 + far) * 2 + core)
    my_rank = jnp.where(is_mid, 1, 0)
    peers = [flip(me, d) for d in range(8)]

    def remote(src, dst, s, r, dev):
        return pltpu.make_async_remote_copy(
            src_ref=src, dst_ref=dst, send_sem=s, recv_sem=r, device_id={"ep": dev}, device_id_type=MESH)

    def raw_copy(ch, j, dev):
        cols = pl.ds(pl.multiple_of(ch * WC, WC), WC)
        return remote(tok.at[:, cols], raw.at[j, ch], raw_s.at[ch], raw_r.at[j, ch], dev)

    def near_copy(ch, d):
        return remote(near.at[d - 1, ch], xb.at[ch, pl.ds(me * pair, pair)],
                      near_s.at[ch, d - 1], x_r.at[ch, me], peers[d])

    def rly_copy(ch, j, d):
        return remote(rly.at[j, d - 1, ch], xb.at[ch, pl.ds(far_src[j] * pair, pair)],
                      rly_s.at[ch, j, d - 1], x_r.at[ch, far_src[j]], peers[d])

    def x_wait(ch, src):
        remote(xb.at[ch, pl.ds(src * pair, pair)], xb.at[ch, pl.ds(src * pair, pair)],
               near_s.at[ch, 0], x_r.at[ch, src], peers[1]).wait_recv()

    def w_copies(i):
        ch, e, slot = i // n_exp, i % n_exp, i % DEPTH
        rws = pl.ds(pl.multiple_of(ch * WC, WC), WC)
        return (pltpu.make_async_copy(wg_hbm.at[e, rws], wg.at[slot], w_s.at[0, slot]),
                pltpu.make_async_copy(wu_hbm.at[e, rws], wu.at[slot], w_s.at[1, slot]))

    def wd_copy(i):
        ch, e, slot = i // n_exp, i % n_exp, i % DEPTH2
        cols = pl.ds(pl.multiple_of(ch * WO, WO), WO)
        return pltpu.make_async_copy(wd_hbm.at[e, :, cols], wd.at[slot], wd_s.at[slot])

    barrier = pltpu.get_barrier_semaphore()
    for d in range(1, 8):
        pl.semaphore_signal(barrier, inc=1, device_id={"ep": peers[d]}, device_id_type=MESH)
    for i in range(DEPTH):
        for c in w_copies(i):
            c.start()
    for i in range(DEPTH2):
        wd_copy(i).start()
    pl.semaphore_wait(barrier, 7)

    raw_copy(0, my_rank, relay_dev).start()

    dev_iota = iota((8, t_dev), 0)
    chosen = jnp.zeros((8, t_dev), F32)
    for j in range(top_k):
        chosen = jnp.where(ids[j:j + 1, :] // n_exp == dev_iota, 1.0, chosen)
    tri = (iota((t_dev, t_dev), 0) <= iota((t_dev, t_dev), 1)).astype(F32).astype(BF16)
    rank = dot(chosen.astype(BF16), tri) - 1.0
    where = jnp.where(chosen > 0.0, rank, FAR)
    pos[...] = where
    pos_copy = remote(pos, rpos.at[my_rank], pos_s, pos_r.at[my_rank], relay_dev)
    pos_copy.start()
    slot_rows = iota((pair, t_dev), 0).astype(F32)
    for q in range(8):
        mat = (slot_rows == where[q:q + 1, :]).astype(F32).astype(BF16)
        pk[q] = mat
        dense = jnp.zeros((n_exp, t_dev), F32)
        for j in range(top_k):
            dense = jnp.where(ids[j:j + 1, :] == q * n_exp + dev_iota, gate[j:j + 1, :], dense)
        parts = dot_nt(split3(dense), mat)
        packed = (parts[n_exp:2 * n_exp] + parts[2 * n_exp:]) + parts[:n_exp]
        gsend[q, :, 0:pair] = packed

    def tab_copy(d):
        return remote(gsend.at[peers[d]], gtab.at[me], tab_s.at[d - 1], tab_r.at[me], peers[d])

    def tab_wait(d):
        remote(gsend.at[peers[d]], gtab.at[peers[d]], tab_s.at[d - 1], tab_r.at[peers[d]], peers[d]).wait_recv()

    for d in range(1, 8):
        tab_copy(d).start()
    gtab[me] = gsend[me]

    def near_step(ch, _):
        cols = pl.ds(pl.multiple_of(ch * WC, WC), WC)
        block = tok[:, cols]
        for d in range(1, 4):
            near[d - 1, ch] = dot(pk[peers[d]], block).astype(BF16)
        xb[ch, pl.ds(me * pair, pair)] = dot(pk[me], block).astype(BF16)

        @pl.when(ch > 0)
        def _():
            raw_copy(ch, my_rank, relay_dev).start()

        for d in (3, 2, 1):
            near_copy(ch, d).start()
        return 0

    lax.fori_loop(0, n_ch, near_step, 0)

    lane = iota((8, rows), 1)
    base = iota((8, rows), 0) * pair
    blocks = ((lane >= base) & (lane < base + pair)).astype(F32).astype(BF16)
    spread = dot_tn(where.astype(BF16), blocks)
    lane_t = iota((t_dev, rows), 1)
    lane_s = lane_t
    for q in range(1, 8):
        lane_s = lane_s - jnp.where(lane_t >= q * pair, pair, 0)
    pt[...] = (spread == lane_s.astype(F32)).astype(F32).astype(BF16)

    def zero(e, _):
        accg[e] = jnp.zeros(accg.shape[1:], F32)
        accu[e] = jnp.zeros(accu.shape[1:], F32)
        return 0

    lax.fori_loop(0, n_exp, zero, 0)

    for d in range(1, 8):
        tab_wait(d)
    gates = jnp.concatenate([gtab[p][:, :pair] for p in range(8)], axis=1)
    member = gates != 0.0
    tri_r = (iota((rows, rows), 0) <= iota((rows, rows), 1)).astype(F32).astype(BF16)
    count = dot(member.astype(F32).astype(BF16), tri_r) - 1.0
    place = jnp.where(member, count, FAR)
    place_b = place.astype(BF16)
    gate_parts = split3(gates)
    cap_rows = iota((cap, rows), 0).astype(F32)
    cap_lanes = iota((rows, cap), 1).astype(F32)
    for e in range(n_exp):
        fan[e] = (cap_rows == place[e:e + 1, :]).astype(F32).astype(BF16)
        pick = (iota((8, cap), 0) == e).astype(F32).astype(BF16)
        fan_t[e] = (dot_tn(place_b, pick) == cap_lanes).astype(F32).astype(BF16)
        pick3 = (lax.rem(iota((24, 128), 0), 8) == e).astype(F32).astype(BF16)
        gb[e] = dot_tn(gate_parts, pick3)

    def pos_wait(j):
        remote(pos, rpos.at[j], pos_s, pos_r.at[j], relay_dev).wait_recv()

    @pl.when(is_mid)
    def _():
        for j in range(2):
            pos_wait(j)

    def relay(ch):
        for j in range(2):
            raw_copy(ch, j, relay_dev).wait_recv()
            block = raw[j, ch]

            def packed(q):
                mat = (slot_rows == rpos[j, pl.ds(q, 1), :]).astype(F32).astype(BF16)
                return dot(mat, block).astype(BF16)

            for d in (3, 2, 1):
                rly[j, d - 1, ch] = packed(peers[d])
                rly_copy(ch, j, d).start()
            xb[ch, pl.ds(far_src[j] * pair, pair)] = packed(me)

    def step_in(ch, _):
        @pl.when(is_mid)
        def _():
            relay(ch)

        for d in range(1, 4):
            x_wait(ch, peers[d])

        @pl.when(is_mid)
        def _():
            for d in (5, 7):
                pass
            x_wait(ch, far_src[0] + 1 - 2 * core)
            x_wait(ch, far_src[1] + 1 - 2 * core)

        @pl.when(jnp.logical_not(is_mid))
        def _():
            for d in range(4, 8):
                x_wait(ch, peers[d])

        def expert(e, _):
            i = ch * n_exp + e
            slot = i % DEPTH
            for c in w_copies(i):
                c.wait()
            xg = dot(fan[e], xb[ch]).astype(BF16)
            accg[e] += dot(xg, wg[slot])
            accu[e] += dot(xg, wu[slot])

            @pl.when(i + DEPTH < n_ch * n_exp)
            def _():
                for c in w_copies(i + DEPTH):
                    c.start()
            return 0

        return lax.fori_loop(0, n_exp, expert, 0)

    lax.fori_loop(0, n_ch, step_in, 0)

    def act(e, _):
        g = accg[e]
        hid[e] = (g / (1.0 + jnp.exp(-g)) * accu[e]).astype(BF16)
        return 0

    lax.fori_loop(0, n_exp, act, 0)

    def ret_copy(ch, d):
        return remote(xb.at[ch, pl.ds(peers[d] * pair, pair)], ret.at[ch, pl.ds(me * pair, pair)],
                      out_s.at[ch, d - 1], ret_r.at[ch, me], peers[d])

    def ret_wait(ch, d):
        src = peers[d]
        remote(xb.at[ch, pl.ds(src * pair, pair)], ret.at[ch, pl.ds(src * pair, pair)],
               out_s.at[ch, d - 1], ret_r.at[ch, src], src).wait_recv()

    def step_out(ch, _):
        def expert(e, _):
            i = ch * n_exp + e
            slot = i % DEPTH2
            wd_copy(i).wait()
            y = dot(hid[e], wd[slot]).astype(BF16)
            z = dot(fan_t[e], y)
            g = gb[e]
            add = jnp.concatenate([g * z[:, k * 128:(k + 1) * 128] for k in range(WO // 128)], axis=1)

            @pl.when(e == 0)
            def _():
                ssum[...] = add

            @pl.when(e > 0)
            def _():
                ssum[...] += add

            @pl.when(i + DEPTH2 < n_out * n_exp)
            def _():
                wd_copy(i + DEPTH2).start()
            return 0

        lax.fori_loop(0, n_exp, expert, 0)
        xb[ch] = ssum[...].astype(BF16)
        ret[ch, pl.ds(me * pair, pair)] = ssum[pl.ds(me * pair, pair)].astype(BF16)
        for d in (7, 6, 5, 4, 3, 2, 1):
            ret_copy(ch, d).start()
        return 0

    def drain(ch, _):
        raw_copy(ch, my_rank, relay_dev).wait_send()
        for d in range(1, 4):
            near_copy(ch, d).wait_send()

        @pl.when(is_mid)
        def _():
            for j in range(2):
                for d in range(1, 4):
                    rly_copy(ch, j, d).wait_send()
        return 0

    lax.fori_loop(0, n_out, step_out, 0)
    lax.fori_loop(0, n_ch, drain, 0)
    pos_copy.wait_send()
    for d in range(1, 8):
        tab_copy(d).wait_send()

    def step_end(ch, _):
        for d in range(1, 8):
            ret_wait(ch, d)
        cols = pl.ds(pl.multiple_of(ch * WO, WO), WO)
        out[:, cols] = (tok[:, cols].astype(F32) + dot(pt[...], ret[ch])).astype(BF16)
        return 0

    lax.fori_loop(0, n_out, step_end, 0)

    def drain_out(ch, _):
        for d in range(1, 8):
            ret_copy(ch, d).wait_send()
        return 0

    lax.fori_loop(0, n_out, drain_out, 0)


def solution(mesh):
    groups = mesh.shape['ep']
    row_spec = P(('dp', 'ep'))
    expert_spec = P('ep')

    def device_step(tokens, expert_ids, gate_vals, w_gate, w_up, w_down):
        t_dev, top_k = expert_ids.shape
        d_model = tokens.shape[1]
        n_exp, _, ffn = w_gate.shape
        pair = t_dev * (top_k // 2) // groups
        cap = t_dev * top_k // n_exp
        rows = groups * pair
        n_ch, n_out = d_model // WC, d_model // WO
        vmem = pl.BlockSpec(memory_space=pltpu.VMEM)
        hbm = pl.BlockSpec(memory_space=pl.ANY)
        dma = pltpu.SemaphoreType.DMA
        return pl.pallas_call(
            kernel,
            out_shape=jax.ShapeDtypeStruct((t_dev, d_model), BF16),
            in_specs=[vmem, vmem, vmem, hbm, hbm, hbm],
            out_specs=vmem,
            scratch_shapes=[
                pltpu.VMEM((3, n_ch, pair, WC), BF16),
                pltpu.VMEM((2, n_ch, t_dev, WC), BF16),
                pltpu.VMEM((2, 3, n_ch, pair, WC), BF16),
                pltpu.VMEM((n_ch, rows, WC), BF16),
                pltpu.VMEM((n_out, rows, WO), BF16),
                pltpu.VMEM((n_exp, cap, ffn), F32),
                pltpu.VMEM((n_exp, cap, ffn), F32),
                pltpu.VMEM((n_exp, cap, ffn), BF16),
                pltpu.VMEM((n_exp, cap, rows), BF16),
                pltpu.VMEM((n_exp, rows, cap), BF16),
                pltpu.VMEM((n_exp, rows, 128), F32),
                pltpu.VMEM((rows, WO), F32),
                pltpu.VMEM((groups, pair, t_dev), BF16),
                pltpu.VMEM((t_dev, rows), BF16),
                pltpu.VMEM((8, t_dev), F32),
                pltpu.VMEM((2, 8, t_dev), F32),
                pltpu.VMEM((groups, n_exp, 128), F32),
                pltpu.VMEM((groups, n_exp, 128), F32),
                pltpu.VMEM((DEPTH, WC, ffn), BF16),
                pltpu.VMEM((DEPTH, WC, ffn), BF16),
                pltpu.VMEM((DEPTH2, ffn, WO), BF16),
                dma((n_ch,)), dma((2, n_ch)), dma((n_ch, 3)), dma((n_ch, 2, 3)), dma((n_ch, groups)),
                dma((7,)), dma((groups,)), dma, dma((2,)),
                dma((n_out, 7)), dma((n_out, groups)), dma((2, DEPTH)), dma((DEPTH2,)),
            ],
            compiler_params=pltpu.CompilerParams(
                collective_id=0, has_side_effects=True, vmem_limit_bytes=67043328),
        )(tokens, expert_ids.T, gate_vals.T, w_gate, w_up, w_down)

    return jax.shard_map(device_step, mesh=mesh, in_specs=(row_spec, row_spec, row_spec, expert_spec, expert_spec, expert_spec), out_specs=row_spec, check_vma=False)
```

time: 246 us -> 173 us (0.70)
  Pallas kernels: 0 us -> 170 us
  matrix products: 84.4 us -> 0 us
  blocking collectives: 74.2 us -> 0 us
  waiting for transfers between devices: 70.4 us -> 0 us
  starting transfers between devices: 10.2 us -> 0 us
  other arithmetic: 5.28 us -> 0 us
    pallas_call x0 -> x1, Pallas kernels: none -> 170 us  [device_step(): pl.pallas_call(kernel, out_shape=jax.ShapeDtypeStruct((t_dev, d_model), B...]
    dot_general x6 -> x0, matrix products: 84.4 us -> none  [the longest x1 25.2 us: expert_ffn(): jnp.einsum('lcd,ldf->lcf', expert_in, w_up, preferred_element_type=jnp.fl...]
    all_to_all x1 -> x0, blocking collectives: 74.2 us -> none  [device_step(): lax.all_to_all(dev_sum.reshape(groups, pair_cap, d_model), 'ep', 0, 0, ti...]
    all_to_all x2 -> x0, waiting for transfers between devices: 70.4 us -> none  [the longest x1 68.7 us: device_step(): recv_rows = lax.all_to_all(send_rows, 'ep', 0, 0, tiled=True)]
    all_to_all x2 -> x0, starting transfers between devices: 10.2 us -> none  [the longest x1 6.39 us: device_step(): recv_gate = lax.all_to_all(send_gate, 'ep', 0, 0, tiled=True)]
    another operation x6 -> x0, other arithmetic: 2.51 us -> none
  transfers between devices with their start and end apart: 2 -> 0, of which waited for: 2 -> 0; matrix products, arithmetic and copies ran while one was open for 3% -> 0% of each run, Pallas kernels for 0% -> 0%
where the time goes in v1:
time: 173 us
  Pallas kernels  170 us (98%)
  local copies, waits for them, and re-layouts  2.3 us (1%)
    pallas_call x1, Pallas kernels, device_step(): pl.pallas_call(kernel, out_shape=jax.ShapeDtypeStruct((t_dev, d_model), B...  170 us

profile of v1, /device:TPU:0, one launch (start us, length us, event | category | flops | bytes accessed | tf_op | source)
XLA Modules:
  0.0 172.8 jit_solution(5473904898328513446)
XLA Ops:
  0.0 170.5 %shard_map.64 = bf16[256,2048]{1,0:T(8,128)(2,1)} custom-call(bf16[256,2048]{1,0:T(8,128)(2,1)} %tok.1, s32[6,256]{1,0:T(8,128)} %bitcast.2, f32[6,256]{1,0:T(8,128)} %bitcast.3, bf16[8,2048,1408]{2,1,0:T(8,128)(2,1)} %wg_hbm.1, bf16[8,2048,1408]{2,1,0:T(8,128)(2,1)} %wu_hbm.1, bf16[8,1408,2048]{2,1,0:T(8,128)(2,1)} %wd_hbm.1), custom_call_target="tpu_custom_call" | custom-call | tf_op jit(solution)/shard_map/pallas_call | solution.py:361
  170.5 2.3 %copy.8 = bf16[256,2048]{1,0:T(8,128)(2,1)} copy(bf16[256,2048]{1,0:T(8,128)(2,1)} %shard_map.64) | data formatting | bytes 2097152

commit v2 on v1

--- a/solution.py
+++ b/solution.py
@@ -11,8 +11,12 @@
 F32, BF16 = jnp.float32, jnp.bfloat16
 WC = 256
 WO = 256
-DEPTH = 4
-DEPTH2 = 6
+DEPTH = 8
+DEPTH2 = 8
+RELAYED = 6
+AHEAD = 3
+UNROLL = 2
+UNROLL2 = 4
 FAR = 255.0
 
 
@@ -52,11 +56,10 @@
 
 
 def kernel(tok, ids, gate, wg_hbm, wu_hbm, wd_hbm, out,
-           near, raw, rly, xb, ret, accg, accu, hid, fan, fan_t, gb, ssum, pk, pt, pos, rpos, gsend, gtab,
-           wg, wu, wd,
-           raw_s, raw_r, near_s, rly_s, x_r, tab_s, tab_r, pos_s, pos_r, out_s, ret_r, w_s, wd_s):
-    n_exp = accg.shape[0]
-    cap = accg.shape[1]
+           near, direct, raw, rly, xb, ret, acc, hid, xg, fan, fan_t, gb, ssum, pk, pt, pos, rpos, gsend, gtab,
+           wgu, wd,
+           raw_s, raw_r, near_s, far_s, rly_s, x_r, tab_s, tab_r, pos_s, pos_r, out_s, ret_r, w_s, wd_s):
+    n_exp, cap, ffn = hid.shape
     t_dev = tok.shape[0]
     n_ch, rows, _ = xb.shape
     n_out = ret.shape[0]
@@ -86,6 +89,10 @@
         return remote(near.at[d - 1, ch], xb.at[ch, pl.ds(me * pair, pair)],
                       near_s.at[ch, d - 1], x_r.at[ch, me], peers[d])
 
+    def far_copy(ch, d):
+        return remote(direct.at[d - 4, ch - RELAYED], xb.at[ch, pl.ds(me * pair, pair)],
+                      far_s.at[ch - RELAYED, d - 4], x_r.at[ch, me], peers[d])
+
     def rly_copy(ch, j, d):
         return remote(rly.at[j, d - 1, ch], xb.at[ch, pl.ds(far_src[j] * pair, pair)],
                       rly_s.at[ch, j, d - 1], x_r.at[ch, far_src[j]], peers[d])
@@ -97,8 +104,8 @@
     def w_copies(i):
         ch, e, slot = i // n_exp, i % n_exp, i % DEPTH
         rws = pl.ds(pl.multiple_of(ch * WC, WC), WC)
-        return (pltpu.make_async_copy(wg_hbm.at[e, rws], wg.at[slot], w_s.at[0, slot]),
-                pltpu.make_async_copy(wu_hbm.at[e, rws], wu.at[slot], w_s.at[1, slot]))
+        return (pltpu.make_async_copy(wg_hbm.at[e, rws], wgu.at[slot, :, pl.ds(0, ffn)], w_s.at[0, slot]),
+                pltpu.make_async_copy(wu_hbm.at[e, rws], wgu.at[slot, :, pl.ds(ffn, ffn)], w_s.at[1, slot]))
 
     def wd_copy(i):
         ch, e, slot = i // n_exp, i % n_exp, i % DEPTH2
@@ -111,11 +118,6 @@
     for i in range(DEPTH):
         for c in w_copies(i):
             c.start()
-    for i in range(DEPTH2):
-        wd_copy(i).start()
-    pl.semaphore_wait(barrier, 7)
-
-    raw_copy(0, my_rank, relay_dev).start()
 
     dev_iota = iota((8, t_dev), 0)
     chosen = jnp.zeros((8, t_dev), F32)
@@ -126,7 +128,6 @@
     where = jnp.where(chosen > 0.0, rank, FAR)
     pos[...] = where
     pos_copy = remote(pos, rpos.at[my_rank], pos_s, pos_r.at[my_rank], relay_dev)
-    pos_copy.start()
     slot_rows = iota((pair, t_dev), 0).astype(F32)
     for q in range(8):
         mat = (slot_rows == where[q:q + 1, :]).astype(F32).astype(BF16)
@@ -144,43 +145,40 @@
     def tab_wait(d):
         remote(gsend.at[peers[d]], gtab.at[peers[d]], tab_s.at[d - 1], tab_r.at[peers[d]], peers[d]).wait_recv()
 
-    for d in range(1, 8):
+    pl.semaphore_wait(barrier, 7)
+    pos_copy.start()
+    for d in (7, 6, 5, 4, 3, 2, 1):
         tab_copy(d).start()
     gtab[me] = gsend[me]
+
+    def near_send(ch):
+        for d in (3, 2, 1):
+            near_copy(ch, d).start()
 
     def near_step(ch, _):
         cols = pl.ds(pl.multiple_of(ch * WC, WC), WC)
         block = tok[:, cols]
+
+        @pl.when(ch < RELAYED)
+        def _():
+            raw_copy(ch, my_rank, relay_dev).start()
+
+        @pl.when(ch >= RELAYED)
+        def _():
+            for d in (7, 6, 5, 4):
+                direct[d - 4, ch - RELAYED] = dot(pk[peers[d]], block).astype(BF16)
+                far_copy(ch, d).start()
+
         for d in range(1, 4):
             near[d - 1, ch] = dot(pk[peers[d]], block).astype(BF16)
         xb[ch, pl.ds(me * pair, pair)] = dot(pk[me], block).astype(BF16)
 
-        @pl.when(ch > 0)
-        def _():
-            raw_copy(ch, my_rank, relay_dev).start()
-
-        for d in (3, 2, 1):
-            near_copy(ch, d).start()
+        @pl.when(jnp.logical_not(is_mid) | (ch < AHEAD))
+        def _():
+            near_send(ch)
         return 0
 
     lax.fori_loop(0, n_ch, near_step, 0)
-
-    lane = iota((8, rows), 1)
-    base = iota((8, rows), 0) * pair
-    blocks = ((lane >= base) & (lane < base + pair)).astype(F32).astype(BF16)
-    spread = dot_tn(where.astype(BF16), blocks)
-    lane_t = iota((t_dev, rows), 1)
-    lane_s = lane_t
-    for q in range(1, 8):
-        lane_s = lane_s - jnp.where(lane_t >= q * pair, pair, 0)
-    pt[...] = (spread == lane_s.astype(F32)).astype(F32).astype(BF16)
-
-    def zero(e, _):
-        accg[e] = jnp.zeros(accg.shape[1:], F32)
-        accu[e] = jnp.zeros(accu.shape[1:], F32)
-        return 0
-
-    lax.fori_loop(0, n_exp, zero, 0)
 
     for d in range(1, 8):
         tab_wait(d)
@@ -189,16 +187,9 @@
     tri_r = (iota((rows, rows), 0) <= iota((rows, rows), 1)).astype(F32).astype(BF16)
     count = dot(member.astype(F32).astype(BF16), tri_r) - 1.0
     place = jnp.where(member, count, FAR)
-    place_b = place.astype(BF16)
-    gate_parts = split3(gates)
     cap_rows = iota((cap, rows), 0).astype(F32)
-    cap_lanes = iota((rows, cap), 1).astype(F32)
     for e in range(n_exp):
         fan[e] = (cap_rows == place[e:e + 1, :]).astype(F32).astype(BF16)
-        pick = (iota((8, cap), 0) == e).astype(F32).astype(BF16)
-        fan_t[e] = (dot_tn(place_b, pick) == cap_lanes).astype(F32).astype(BF16)
-        pick3 = (lax.rem(iota((24, 128), 0), 8) == e).astype(F32).astype(BF16)
-        gb[e] = dot_tn(gate_parts, pick3)
 
     def pos_wait(j):
         remote(pos, rpos.at[j], pos_s, pos_r.at[j], relay_dev).wait_recv()
@@ -222,51 +213,91 @@
                 rly_copy(ch, j, d).start()
             xb[ch, pl.ds(far_src[j] * pair, pair)] = packed(me)
 
-    def step_in(ch, _):
-        @pl.when(is_mid)
+        @pl.when(ch + AHEAD < n_ch)
+        def _():
+            near_send(ch + AHEAD)
+
+    def group(ch, first, last):
+        @pl.when(is_mid & (ch < RELAYED))
         def _():
             relay(ch)
 
         for d in range(1, 4):
             x_wait(ch, peers[d])
 
-        @pl.when(is_mid)
-        def _():
-            for d in (5, 7):
-                pass
-            x_wait(ch, far_src[0] + 1 - 2 * core)
-            x_wait(ch, far_src[1] + 1 - 2 * core)
-
-        @pl.when(jnp.logical_not(is_mid))
+        straight = jnp.logical_not(is_mid) | (ch >= RELAYED)
+
+        @pl.when(jnp.logical_not(straight))
+        def _():
+            for src in far_src:
+                x_wait(ch, src + 1 - 2 * core)
+
+        @pl.when(straight)
         def _():
             for d in range(4, 8):
                 x_wait(ch, peers[d])
 
-        def expert(e, _):
-            i = ch * n_exp + e
-            slot = i % DEPTH
-            for c in w_copies(i):
-                c.wait()
-            xg = dot(fan[e], xb[ch]).astype(BF16)
-            accg[e] += dot(xg, wg[slot])
-            accu[e] += dot(xg, wu[slot])
-
-            @pl.when(i + DEPTH < n_ch * n_exp)
-            def _():
-                for c in w_copies(i + DEPTH):
-                    c.start()
+        block = xb[ch]
+        for e in range(n_exp):
+            xg[e] = dot(fan[e], block).astype(BF16)
+
+        def experts(it, _):
+            for u in range(UNROLL):
+                for c in w_copies(ch * n_exp + it * UNROLL + u):
+                    c.wait()
+            for u in range(UNROLL):
+                e = it * UNROLL + u
+                slot = (ch * n_exp + e) % DEPTH
+                both = dot(xg[e], wgu[slot])
+                if not first:
+                    both = acc[e] + both
+                if last:
+                    g = both[:, :ffn]
+                    hid[e] = (g / (1.0 + jnp.exp(-g)) * both[:, ffn:]).astype(BF16)
+                else:
+                    acc[e] = both
+            if not last:
+                for u in range(UNROLL):
+                    i = ch * n_exp + it * UNROLL + u + DEPTH
+
+                    @pl.when(i < n_ch * n_exp)
+                    def _():
+                        for c in w_copies(i):
+                            c.start()
             return 0
 
-        return lax.fori_loop(0, n_exp, expert, 0)
-
-    lax.fori_loop(0, n_ch, step_in, 0)
-
-    def act(e, _):
-        g = accg[e]
-        hid[e] = (g / (1.0 + jnp.exp(-g)) * accu[e]).astype(BF16)
-        return 0
-
-    lax.fori_loop(0, n_exp, act, 0)
+        lax.fori_loop(0, n_exp // UNROLL, experts, 0)
+
+    def middle_group(ch, _):
+        group(ch, False, False)
+        return 0
+
+    def return_tables():
+        lane = iota((8, rows), 1)
+        base = iota((8, rows), 0) * pair
+        blocks = ((lane >= base) & (lane < base + pair)).astype(F32).astype(BF16)
+        spread = dot_tn(where.astype(BF16), blocks)
+        lane_t = iota((t_dev, rows), 1)
+        lane_s = lane_t
+        for q in range(1, 8):
+            lane_s = lane_s - jnp.where(lane_t >= q * pair, pair, 0)
+        pt[...] = (spread == lane_s.astype(F32)).astype(F32).astype(BF16)
+
+        place_b = place.astype(BF16)
+        gate_parts = split3(gates)
+        cap_lanes = iota((rows, cap), 1).astype(F32)
+        for e in range(n_exp):
+            pick = (iota((8, cap), 0) == e).astype(F32).astype(BF16)
+            fan_t[e] = (dot_tn(place_b, pick) == cap_lanes).astype(F32).astype(BF16)
+            pick3 = (lax.rem(iota((24, 128), 0), 8) == e).astype(F32).astype(BF16)
+            gb[e] = dot_tn(gate_parts, pick3)
+
+    group(0, True, False)
+    for i in range(DEPTH2):
+        wd_copy(i).start()
+    return_tables()
+    lax.fori_loop(1, n_ch - 1, middle_group, 0)
+    group(n_ch - 1, False, True)
 
     def ret_copy(ch, d):
         return remote(xb.at[ch, pl.ds(peers[d] * pair, pair)], ret.at[ch, pl.ds(me * pair, pair)],
@@ -278,29 +309,34 @@
                out_s.at[ch, d - 1], ret_r.at[ch, src], src).wait_recv()
 
     def step_out(ch, _):
-        def expert(e, _):
-            i = ch * n_exp + e
-            slot = i % DEPTH2
-            wd_copy(i).wait()
-            y = dot(hid[e], wd[slot]).astype(BF16)
-            z = dot(fan_t[e], y)
-            g = gb[e]
-            add = jnp.concatenate([g * z[:, k * 128:(k + 1) * 128] for k in range(WO // 128)], axis=1)
-
-            @pl.when(e == 0)
+        def experts(it, _):
+            first = ch * n_exp + it * UNROLL2
+            for u in range(UNROLL2):
+                wd_copy(first + u).wait()
+            ys = [dot(hid[it * UNROLL2 + u], wd[(first + u) % DEPTH2]).astype(BF16) for u in range(UNROLL2)]
+            add = None
+            for u in range(UNROLL2):
+                e = it * UNROLL2 + u
+                z = dot(fan_t[e], ys[u])
+                g = gb[e]
+                part = jnp.concatenate([g * z[:, k * 128:(k + 1) * 128] for k in range(WO // 128)], axis=1)
+                add = part if add is None else add + part
+
+            @pl.when(it == 0)
             def _():
                 ssum[...] = add
 
-            @pl.when(e > 0)
+            @pl.when(it > 0)
             def _():
                 ssum[...] += add
 
-            @pl.when(i + DEPTH2 < n_out * n_exp)
-            def _():
-                wd_copy(i + DEPTH2).start()
+            for u in range(UNROLL2):
+                @pl.when(first + u + DEPTH2 < n_out * n_exp)
+                def _():
+                    wd_copy(first + u + DEPTH2).start()
             return 0
 
-        lax.fori_loop(0, n_exp, expert, 0)
+        lax.fori_loop(0, n_exp // UNROLL2, experts, 0)
         xb[ch] = ssum[...].astype(BF16)
         ret[ch, pl.ds(me * pair, pair)] = ssum[pl.ds(me * pair, pair)].astype(BF16)
         for d in (7, 6, 5, 4, 3, 2, 1):
@@ -308,11 +344,19 @@
         return 0
 
     def drain(ch, _):
-        raw_copy(ch, my_rank, relay_dev).wait_send()
         for d in range(1, 4):
             near_copy(ch, d).wait_send()
 
-        @pl.when(is_mid)
+        @pl.when(ch < RELAYED)
+        def _():
+            raw_copy(ch, my_rank, relay_dev).wait_send()
+
+        @pl.when(ch >= RELAYED)
+        def _():
+            for d in range(4, 8):
+                far_copy(ch, d).wait_send()
+
+        @pl.when(is_mid & (ch < RELAYED))
         def _():
             for j in range(2):
                 for d in range(1, 4):
@@ -365,13 +409,14 @@
             out_specs=vmem,
             scratch_shapes=[
                 pltpu.VMEM((3, n_ch, pair, WC), BF16),
-                pltpu.VMEM((2, n_ch, t_dev, WC), BF16),
-                pltpu.VMEM((2, 3, n_ch, pair, WC), BF16),
+                pltpu.VMEM((4, max(n_ch - RELAYED, 1), pair, WC), BF16),
+                pltpu.VMEM((2, RELAYED, t_dev, WC), BF16),
+                pltpu.VMEM((2, 3, RELAYED, pair, WC), BF16),
                 pltpu.VMEM((n_ch, rows, WC), BF16),
                 pltpu.VMEM((n_out, rows, WO), BF16),
-                pltpu.VMEM((n_exp, cap, ffn), F32),
-                pltpu.VMEM((n_exp, cap, ffn), F32),
+                pltpu.VMEM((n_exp, cap, 2 * ffn), F32),
                 pltpu.VMEM((n_exp, cap, ffn), BF16),
+                pltpu.VMEM((n_exp, cap, WC), BF16),
                 pltpu.VMEM((n_exp, cap, rows), BF16),
                 pltpu.VMEM((n_exp, rows, cap), BF16),
                 pltpu.VMEM((n_exp, rows, 128), F32),
@@ -382,10 +427,9 @@
                 pltpu.VMEM((2, 8, t_dev), F32),
                 pltpu.VMEM((groups, n_exp, 128), F32),
                 pltpu.VMEM((groups, n_exp, 128), F32),
-                pltpu.VMEM((DEPTH, WC, ffn), BF16),
-                pltpu.VMEM((DEPTH, WC, ffn), BF16),
+                pltpu.VMEM((DEPTH, WC, 2 * ffn), BF16),
                 pltpu.VMEM((DEPTH2, ffn, WO), BF16),
-                dma((n_ch,)), dma((2, n_ch)), dma((n_ch, 3)), dma((n_ch, 2, 3)), dma((n_ch, groups)),
+                dma((n_ch,)), dma((2, n_ch)), dma((n_ch, 3)), dma((max(n_ch - RELAYED, 1), 4)), dma((n_ch, 2, 3)), dma((n_ch, groups)),
                 dma((7,)), dma((groups,)), dma, dma((2,)),
                 dma((n_out, 7)), dma((n_out, groups)), dma((2, DEPTH)), dma((DEPTH2,)),
             ],

time: 173 us -> 146 us (0.84)
  Pallas kernels: 170 us -> 143 us
    pallas_call x1, Pallas kernels: 170 us -> 143 us  [device_step(): pl.pallas_call(kernel, out_shape=jax.ShapeDtypeStruct((t_dev, d_model), B...]
where the time goes in v2:
time: 146 us; the launch traced here: 145 us
  Pallas kernels  143 us (98%)
  local copies, waits for them, and re-layouts  2.3 us (2%)
    pallas_call x1, Pallas kernels, device_step(): pl.pallas_call(kernel, out_shape=jax.ShapeDtypeStruct((t_dev, d_model), B...  143 us

profile of v2, /device:TPU:0, one launch (start us, length us, event | category | flops | bytes accessed | tf_op | source)
XLA Modules:
  0.0 145.2 jit_solution(3409216524757380090)
XLA Ops:
  0.0 142.8 %shard_map.64 = bf16[256,2048]{1,0:T(8,128)(2,1)} custom-call(bf16[256,2048]{1,0:T(8,128)(2,1)} %tok.1, s32[6,256]{1,0:T(8,128)} %bitcast.2, f32[6,256]{1,0:T(8,128)} %bitcast.3, bf16[8,2048,1408]{2,1,0:T(8,128)(2,1)} %wg_hbm.1, bf16[8,2048,1408]{2,1,0:T(8,128)(2,1)} %wu_hbm.1, bf16[8,1408,2048]{2,1,0:T(8,128)(2,1)} %wd_hbm.1), custom_call_target="tpu_custom_call" | custom-call | tf_op jit(solution)/shard_map/pallas_call | solution.py:405
  142.8 2.3 %copy.8 = bf16[256,2048]{1,0:T(8,128)(2,1)} copy(bf16[256,2048]{1,0:T(8,128)(2,1)} %shard_map.64) | data formatting | bytes 2097152

commit v3 on v2

--- a/solution.py
+++ b/solution.py
@@ -13,9 +13,9 @@
 WO = 256
 DEPTH = 8
 DEPTH2 = 8
-RELAYED = 6
+RELAYED = 5
 AHEAD = 3
-UNROLL = 2
+UNROLL = 4
 UNROLL2 = 4
 FAR = 255.0
 
@@ -55,10 +55,10 @@
     return jnp.concatenate([hi, mid, rest - mid], axis=0).astype(BF16)
 
 
-def kernel(tok, ids, gate, wg_hbm, wu_hbm, wd_hbm, out,
-           near, direct, raw, rly, xb, ret, acc, hid, xg, fan, fan_t, gb, ssum, pk, pt, pos, rpos, gsend, gtab,
+def kernel(tok_hbm, ids_hbm, gate_hbm, wg_hbm, wu_hbm, wd_hbm, out_hbm,
+           tok, ids, gate, out, near, direct, raw, rly, xb, ret, acc, hid, xg, fan, fan_t, gb, ssum, pk, pt, pos, rpos, gsend, gtab,
            wgu, wd,
-           raw_s, raw_r, near_s, far_s, rly_s, x_r, tab_s, tab_r, pos_s, pos_r, out_s, ret_r, w_s, wd_s):
+           raw_s, raw_r, near_s, far_s, rly_s, x_r, tab_s, tab_r, pos_s, pos_r, out_s, ret_r, w_s, wd_s, in_s, done_s):
     n_exp, cap, ffn = hid.shape
     t_dev = tok.shape[0]
     n_ch, rows, _ = xb.shape
@@ -112,6 +112,10 @@
         cols = pl.ds(pl.multiple_of(ch * WO, WO), WO)
         return pltpu.make_async_copy(wd_hbm.at[e, :, cols], wd.at[slot], wd_s.at[slot])
 
+    loads = [pltpu.make_async_copy(a, b, in_s.at[k]) for k, (a, b) in enumerate(
+        ((ids_hbm, ids), (gate_hbm, gate), (tok_hbm, tok)))]
+    for c in loads:
+        c.start()
     barrier = pltpu.get_barrier_semaphore()
     for d in range(1, 8):
         pl.semaphore_signal(barrier, inc=1, device_id={"ep": peers[d]}, device_id_type=MESH)
@@ -119,6 +123,8 @@
         for c in w_copies(i):
             c.start()
 
+    loads[0].wait()
+    loads[1].wait()
     dev_iota = iota((8, t_dev), 0)
     chosen = jnp.zeros((8, t_dev), F32)
     for j in range(top_k):
@@ -145,6 +151,7 @@
     def tab_wait(d):
         remote(gsend.at[peers[d]], gtab.at[peers[d]], tab_s.at[d - 1], tab_r.at[peers[d]], peers[d]).wait_recv()
 
+    loads[2].wait()
     pl.semaphore_wait(barrier, 7)
     pos_copy.start()
     for d in (7, 6, 5, 4, 3, 2, 1):
@@ -155,6 +162,17 @@
         for d in (3, 2, 1):
             near_copy(ch, d).start()
 
+    def far_send(ch, from_mid, from_end):
+        @pl.when(is_mid)
+        def _():
+            for d in from_mid:
+                far_copy(ch, d).start()
+
+        @pl.when(jnp.logical_not(is_mid))
+        def _():
+            for d in from_end:
+                far_copy(ch, d).start()
+
     def near_step(ch, _):
         cols = pl.ds(pl.multiple_of(ch * WC, WC), WC)
         block = tok[:, cols]
@@ -167,7 +185,7 @@
         def _():
             for d in (7, 6, 5, 4):
                 direct[d - 4, ch - RELAYED] = dot(pk[peers[d]], block).astype(BF16)
-                far_copy(ch, d).start()
+            far_send(ch, (7, 6), (5, 4))
 
         for d in range(1, 4):
             near[d - 1, ch] = dot(pk[peers[d]], block).astype(BF16)
@@ -179,6 +197,8 @@
         return 0
 
     lax.fori_loop(0, n_ch, near_step, 0)
+    for ch in range(RELAYED, n_ch):
+        far_send(ch, (5, 4), (7, 6))
 
     for d in range(1, 8):
         tab_wait(d)
@@ -256,8 +276,6 @@
                     hid[e] = (g / (1.0 + jnp.exp(-g)) * both[:, ffn:]).astype(BF16)
                 else:
                     acc[e] = both
-            if not last:
-                for u in range(UNROLL):
                     i = ch * n_exp + it * UNROLL + u + DEPTH
 
                     @pl.when(i < n_ch * n_exp)
@@ -369,11 +387,16 @@
     for d in range(1, 8):
         tab_copy(d).wait_send()
 
+    def done_copy(ch):
+        cols = pl.ds(pl.multiple_of(ch * WO, WO), WO)
+        return pltpu.make_async_copy(out.at[ch], out_hbm.at[:, cols], done_s.at[ch])
+
     def step_end(ch, _):
         for d in range(1, 8):
             ret_wait(ch, d)
         cols = pl.ds(pl.multiple_of(ch * WO, WO), WO)
-        out[:, cols] = (tok[:, cols].astype(F32) + dot(pt[...], ret[ch])).astype(BF16)
+        out[ch] = (tok[:, cols].astype(F32) + dot(pt[...], ret[ch])).astype(BF16)
+        done_copy(ch).start()
         return 0
 
     lax.fori_loop(0, n_out, step_end, 0)
@@ -381,6 +404,7 @@
     def drain_out(ch, _):
         for d in range(1, 8):
             ret_copy(ch, d).wait_send()
+        done_copy(ch).wait()
         return 0
 
     lax.fori_loop(0, n_out, drain_out, 0)
@@ -399,15 +423,18 @@
         cap = t_dev * top_k // n_exp
         rows = groups * pair
         n_ch, n_out = d_model // WC, d_model // WO
-        vmem = pl.BlockSpec(memory_space=pltpu.VMEM)
         hbm = pl.BlockSpec(memory_space=pl.ANY)
         dma = pltpu.SemaphoreType.DMA
         return pl.pallas_call(
             kernel,
             out_shape=jax.ShapeDtypeStruct((t_dev, d_model), BF16),
-            in_specs=[vmem, vmem, vmem, hbm, hbm, hbm],
-            out_specs=vmem,
+            in_specs=[hbm] * 6,
+            out_specs=hbm,
             scratch_shapes=[
+                pltpu.VMEM((t_dev, d_model), BF16),
+                pltpu.VMEM((top_k, t_dev), jnp.int32),
+                pltpu.VMEM((top_k, t_dev), F32),
+                pltpu.VMEM((n_out, t_dev, WO), BF16),
                 pltpu.VMEM((3, n_ch, pair, WC), BF16),
                 pltpu.VMEM((4, max(n_ch - RELAYED, 1), pair, WC), BF16),
                 pltpu.VMEM((2, RELAYED, t_dev, WC), BF16),
@@ -432,6 +459,7 @@
                 dma((n_ch,)), dma((2, n_ch)), dma((n_ch, 3)), dma((max(n_ch - RELAYED, 1), 4)), dma((n_ch, 2, 3)), dma((n_ch, groups)),
                 dma((7,)), dma((groups,)), dma, dma((2,)),
                 dma((n_out, 7)), dma((n_out, groups)), dma((2, DEPTH)), dma((DEPTH2,)),
+                dma((3,)), dma((n_out,)),
             ],
             compiler_params=pltpu.CompilerParams(
                 collective_id=0, has_side_effects=True, vmem_limit_bytes=67043328),

time: 146 us -> 141 us (0.966)
  Pallas kernels: 143 us -> 138 us
    pallas_call x1, Pallas kernels: 143 us -> 138 us  [device_step(): pl.pallas_call(kernel, out_shape=jax.ShapeDtypeStruct((t_dev, d_model), B...]
where the time goes in v3:
time: 141 us; the launch traced here: 140 us
  Pallas kernels  138 us (98%)
  local copies, waits for them, and re-layouts  2.3 us (2%)
    pallas_call x1, Pallas kernels, device_step(): pl.pallas_call(kernel, out_shape=jax.ShapeDtypeStruct((t_dev, d_model), B...  138 us

profile of v3, /device:TPU:0, one launch (start us, length us, event | category | flops | bytes accessed | tf_op | source)
XLA Modules:
  0.0 140.3 jit_solution(10862279919771216017)
XLA Ops:
  0.0 138.0 %shard_map.64 = bf16[256,2048]{1,0:T(8,128)(2,1)} custom-call(bf16[256,2048]{1,0:T(8,128)(2,1)} %tok_hbm.1, s32[6,256]{1,0:T(8,128)} %bitcast.2, f32[6,256]{1,0:T(8,128)} %bitcast.3, bf16[8,2048,1408]{2,1,0:T(8,128)(2,1)} %wg_hbm.1, bf16[8,2048,1408]{2,1,0:T(8,128)(2,1)} %wu_hbm.1, bf16[8,1408,2048]{2,1,0:T(8,128)(2,1)} %wd_hbm.1), custom_call_target="tpu_custom_call" | custom-call | tf_op jit(solution)/shard_map/pallas_call | solution.py:428
  138.0 2.3 %copy.8 = bf16[256,2048]{1,0:T(8,128)(2,1)} copy(bf16[256,2048]{1,0:T(8,128)(2,1)} %shard_map.64) | data formatting | bytes 2097152

commit v4 on v3

--- a/solution.py
+++ b/solution.py
@@ -13,10 +13,11 @@
 WO = 256
 DEPTH = 8
 DEPTH2 = 8
-RELAYED = 5
-AHEAD = 3
+RELAYED = 4
+AHEAD = 4
+LATE = 4
 UNROLL = 4
-UNROLL2 = 4
+UNROLL2 = 8
 FAR = 255.0
 
 
@@ -83,7 +84,7 @@
 
     def raw_copy(ch, j, dev):
         cols = pl.ds(pl.multiple_of(ch * WC, WC), WC)
-        return remote(tok.at[:, cols], raw.at[j, ch], raw_s.at[ch], raw_r.at[j, ch], dev)
+        return remote(tok_hbm.at[:, cols], raw.at[j, ch], raw_s.at[ch], raw_r.at[j, ch], dev)
 
     def near_copy(ch, d):
         return remote(near.at[d - 1, ch], xb.at[ch, pl.ds(me * pair, pair)],
@@ -119,6 +120,8 @@
     barrier = pltpu.get_barrier_semaphore()
     for d in range(1, 8):
         pl.semaphore_signal(barrier, inc=1, device_id={"ep": peers[d]}, device_id_type=MESH)
+    pl.semaphore_wait(barrier, 7)
+    raw_copy(0, my_rank, relay_dev).start()
     for i in range(DEPTH):
         for c in w_copies(i):
             c.start()
@@ -151,8 +154,6 @@
     def tab_wait(d):
         remote(gsend.at[peers[d]], gtab.at[peers[d]], tab_s.at[d - 1], tab_r.at[peers[d]], peers[d]).wait_recv()
 
-    loads[2].wait()
-    pl.semaphore_wait(barrier, 7)
     pos_copy.start()
     for d in (7, 6, 5, 4, 3, 2, 1):
         tab_copy(d).start()
@@ -177,7 +178,7 @@
         cols = pl.ds(pl.multiple_of(ch * WC, WC), WC)
         block = tok[:, cols]
 
-        @pl.when(ch < RELAYED)
+        @pl.when((ch > 0) & (ch < RELAYED))
         def _():
             raw_copy(ch, my_rank, relay_dev).start()
 
@@ -196,9 +197,10 @@
             near_send(ch)
         return 0
 
+    loads[2].wait()
     lax.fori_loop(0, n_ch, near_step, 0)
     for ch in range(RELAYED, n_ch):
-        far_send(ch, (5, 4), (7, 6))
+        far_send(ch, (5, 4), ())
 
     for d in range(1, 8):
         tab_wait(d)
@@ -287,6 +289,11 @@
         lax.fori_loop(0, n_exp // UNROLL, experts, 0)
 
     def middle_group(ch, _):
+        @pl.when(ch == LATE)
+        def _():
+            for k in range(RELAYED, n_ch):
+                far_send(k, (), (7, 6))
+
         group(ch, False, False)
         return 0
 

time: 141 us -> 139 us (0.986)
    pallas_call x1, Pallas kernels: 138 us -> 137 us  [device_step(): pl.pallas_call(kernel, out_shape=jax.ShapeDtypeStruct((t_dev, d_model), B...]
where the time goes in v4:
time: 139 us
  Pallas kernels  137 us (99%)
  local copies, waits for them, and re-layouts  2.3 us (2%)
    pallas_call x1, Pallas kernels, device_step(): pl.pallas_call(kernel, out_shape=jax.ShapeDtypeStruct((t_dev, d_model), B...  137 us

profile of v4, /device:TPU:0, one launch (start us, length us, event | category | flops | bytes accessed | tf_op | source)
XLA Modules:
  0.0 138.9 jit_solution(8529536316611103729)
XLA Ops:
  0.0 136.5 %shard_map.64 = bf16[256,2048]{1,0:T(8,128)(2,1)} custom-call(bf16[256,2048]{1,0:T(8,128)(2,1)} %tok_hbm.1, s32[6,256]{1,0:T(8,128)} %bitcast.2, f32[6,256]{1,0:T(8,128)} %bitcast.3, bf16[8,2048,1408]{2,1,0:T(8,128)(2,1)} %wg_hbm.1, bf16[8,2048,1408]{2,1,0:T(8,128)(2,1)} %wu_hbm.1, bf16[8,1408,2048]{2,1,0:T(8,128)(2,1)} %wd_hbm.1), custom_call_target="tpu_custom_call" | custom-call | tf_op jit(solution)/shard_map/pallas_call | solution.py:435
  136.6 2.3 %copy.8 = bf16[256,2048]{1,0:T(8,128)(2,1)} copy(bf16[256,2048]{1,0:T(8,128)(2,1)} %shard_map.64) | data formatting | bytes 2097152
